TPU v7x, 32 devices: a whole 2x2x4 slice. The times are simulated.
32 devices in a mesh: ctx: 4 (over x, core), exp: 8 (over z, y).
Axes of the slice: x: 2, y: 2, z: 4, core: 2. Of those that a mesh axis runs over, the one named last changes fastest.
Arguments:
- q_nope: bfloat16 [128, 128, 512], P('ctx', 'exp'), may hold values from -72 to 72
- q_rope: bfloat16 [128, 8192], P('ctx', 'exp'), may hold values from -6 to 6
- cache_keys: bfloat16 [576, 512], P(None, 'ctx'), may hold values from -6 to 6
- fresh_keys: bfloat16 [576, 128], P(None, 'ctx'), may hold values from -6 to 6
- block_order: int32 [8], replicated, may hold values from 0 to 7, each once
- w_uv: bfloat16 [128, 512, 128], P('exp'), may hold values from -0.25 to 0.25
- w_out: bfloat16 [16384, 7168], P('exp', 'ctx'), may hold values from -0.046875 to 0.046875
- residual: bfloat16 [128, 7168], P(('ctx', 'exp')), may hold values from -6 to 6
- norm_gain: float32 [7168], replicated, may hold values from 0.5 to 1.5
- router_weight: bfloat16 [7168, 16], replicated, may hold values from -0.0625 to 0.0625
- expert_ids: int32 [128, 8], P(('ctx', 'exp')), may hold values from 0 to 15, all different within a row; in each aligned block of 4 rows (0 to 3, 4 to 7, ...) at most 3 rows name the same one
- w_gate: bfloat16 [16, 7168, 2048], P('exp', None, 'ctx'), may hold values from -0.0625 to 0.0625
- w_up: bfloat16 [16, 7168, 2048], P('exp', None, 'ctx'), may hold values from -0.0625 to 0.0625
- w_down: bfloat16 [16, 2048, 7168], P('exp', 'ctx'), may hold values from -0.125 to 0.125
Outputs:
- layer_out: bfloat16 [128, 7168], P(('ctx', 'exp'))
Inputs may be any that keep to these rules, and one draw needn't show every extreme that they name: A permutation: block j of the new tokens (16 rows) sits at positions 512 + block_order[j] * 16 onward. `expert_ids`: each row names 8 different experts; the 4 rows of one device name no expert more than 3 times, and in some aligned block one expert exactly 3 times.
All inputs are finite; a program needn't handle non-finite values.
Results may differ from a plain program's by a relative error of at most 0.012.
Values may be sent and summed in bfloat16 or wider, within the bound.
A program may use at most 128 MiB of HBM per device.

v0:
```python
import math
import jax
import jax.numpy as jnp
from jax import lax
from jax.sharding import PartitionSpec as P

QKD = 192
CAP = 3
ROUTE_SCALE = 2.5
NORM_EPS = 1e-06


def block_position(row_index, block_order, block_rows):
    blocks = row_index // block_rows
    lookup = blocks[:, None] == jnp.arange(block_order.shape[0], dtype=jnp.int32)[None, :]
    leading = jnp.sum(jnp.where(lookup, block_order[None, :], 0), axis=1)
    return leading * block_rows + row_index % block_rows


def attend(query_lat, query_pe, keys, visible):
    row_count, head_count, latent_width = query_lat.shape
    key_count = keys.shape[1]
    pe_width = query_pe.shape[1] // head_count
    first_dot = jnp.dot(
        query_lat.reshape(row_count * head_count, latent_width),
        keys[:latent_width],
        preferred_element_type=jnp.float32,
    )
    second_dot = jnp.dot(
        query_pe.reshape(row_count * head_count, pe_width),
        keys[latent_width:],
        preferred_element_type=jnp.float32,
    )
    scores = ((first_dot + second_dot) * (1.0 / math.sqrt(QKD))).reshape(
        row_count, head_count, key_count
    )
    scores = jnp.where(visible[:, None, :], scores, -jnp.inf)
    row_max = jnp.max(scores, axis=2)
    exponent = jnp.exp(scores - row_max[:, :, None])
    row_sum = jnp.sum(exponent, axis=2)
    weights = exponent.astype(jnp.bfloat16).reshape(row_count * head_count, key_count)
    latent = lax.dot_general(
        weights, keys[:latent_width], (((1,), (1,)), ((), ())), preferred_element_type=jnp.float32
    )
    return (row_max, row_sum, latent.reshape(row_count, head_count, latent_width))


def merge_partial(earlier, latter):
    highest = latter[0]
    earlier_scale = jnp.exp(earlier[0] - highest)
    latter_scale = jnp.exp(latter[0] - highest)
    row_sum = earlier_scale * earlier[1] + latter_scale * latter[1]
    latent = earlier_scale[:, :, None] * earlier[2] + latter_scale[:, :, None] * latter[2]
    return (highest, row_sum, latent)


def body(
    q_nope,
    q_rope,
    cache_keys,
    fresh_keys,
    block_order,
    w_uv,
    w_out,
    residual,
    norm_gain,
    router_weight,
    expert_ids,
    w_gate,
    w_up,
    w_down,
):
    ctx_count = lax.axis_size("ctx")
    exp_count = lax.axis_size("exp")
    ctx_index = lax.axis_index("ctx")
    rows_here, heads_here, latent_width = q_nope.shape
    value_width = w_uv.shape[2]
    cache_len = cache_keys.shape[1]
    key_cols = cache_len + rows_here
    block_rows = rows_here // 2
    keys_here = jnp.concatenate([cache_keys, fresh_keys], axis=1)
    w_uv_wide = w_uv.astype(jnp.float32)
    own_rows = ctx_index * rows_here + jnp.arange(rows_here, dtype=jnp.int32)
    own_pos = block_position(own_rows, block_order, block_rows)
    start_state = (
        jnp.full((rows_here, heads_here), -jnp.inf, jnp.float32),
        jnp.zeros((rows_here, heads_here), jnp.float32),
        jnp.zeros((rows_here, heads_here, latent_width), jnp.float32),
    )
    portion = lax.all_gather(keys_here, "ctx", axis=1, tiled=True)
    columns = jnp.arange(portion.shape[1], dtype=jnp.int32)
    owner_dev = columns // key_cols
    within = columns % key_cols
    fresh_row = owner_dev * rows_here + within - cache_len
    key_pos = jnp.where(within < cache_len, -1, block_position(fresh_row, block_order, block_rows))
    visible = key_pos[None, :] <= own_pos[:, None]
    row_max, row_sum, latent = merge_partial(start_state, attend(q_nope, q_rope, portion, visible))
    normal_lat = latent / row_sum[:, :, None]
    head_wide = jnp.einsum("rhl,hlv->rhv", normal_lat, w_uv_wide, precision=lax.Precision.HIGHEST)
    head_out = head_wide.astype(jnp.bfloat16).reshape(rows_here, heads_here * value_width)
    tok_here, model_width = residual.shape
    col_part = w_out.shape[1]
    head_partial = jnp.dot(
        lax.all_gather(head_out, "ctx", axis=0, tiled=True),
        w_out,
        preferred_element_type=jnp.float32,
    )
    arranged = head_partial.reshape(ctx_count, exp_count, tok_here, col_part)
    head_total = lax.psum_scatter(
        arranged.astype(jnp.bfloat16), "exp", scatter_dimension=1, tiled=True
    )
    attention = lax.all_to_all(head_total, "ctx", split_axis=0, concat_axis=3, tiled=True).reshape(
        tok_here, model_width
    )
    hidden = residual.astype(jnp.float32) + attention.astype(jnp.float32)
    mean_square = jnp.mean(hidden * hidden, axis=1, keepdims=True)
    normed = (hidden * lax.rsqrt(mean_square + NORM_EPS) * norm_gain).astype(jnp.bfloat16)
    affinity = jax.nn.sigmoid(jnp.dot(normed, router_weight, preferred_element_type=jnp.float32))
    expert_count = router_weight.shape[1]
    onehot = expert_ids[:, :, None] == jnp.arange(expert_count, dtype=jnp.int32)[None, None, :]
    chosen = jnp.sum(jnp.where(onehot, affinity[:, None, :], 0.0), axis=2)
    route = ROUTE_SCALE * chosen / jnp.sum(chosen, axis=1, keepdims=True)
    mixing = jnp.sum(jnp.where(onehot, route[:, :, None], 0.0), axis=1)
    picked = jnp.sum(onehot.astype(jnp.int32), axis=1)
    slot_index = jnp.cumsum(picked, axis=0) - picked
    slot_hot = (slot_index[:, :, None] == jnp.arange(CAP, dtype=jnp.int32)[None, None, :]) & (
        picked[:, :, None] > 0
    )
    dispatch_map = (
        jnp.transpose(slot_hot, (1, 2, 0))
        .reshape(expert_count * CAP, tok_here)
        .astype(jnp.bfloat16)
    )
    send_rows = jnp.dot(dispatch_map, normed, preferred_element_type=jnp.float32).astype(
        jnp.bfloat16
    )
    arrived = lax.all_to_all(
        send_rows.reshape(expert_count, CAP, model_width),
        "exp",
        split_axis=0,
        concat_axis=1,
        tiled=True,
    )
    local_experts = arrived.shape[0]
    portion = lax.all_gather(arrived, "ctx", axis=1, tiled=True)
    gate = jnp.einsum("end,edf->enf", portion, w_gate, preferred_element_type=jnp.float32)
    upward = jnp.einsum("end,edf->enf", portion, w_up, preferred_element_type=jnp.float32)
    activations = (jax.nn.silu(gate) * upward).astype(jnp.bfloat16)
    expert_total = lax.psum_scatter(
        jnp.einsum("enf,efd->ned", activations, w_down, preferred_element_type=jnp.float32).astype(
            jnp.bfloat16
        ),
        "ctx",
        scatter_dimension=0,
        tiled=True,
    )
    going_back = expert_total.reshape(exp_count, CAP, local_experts, model_width)
    returned = lax.all_to_all(going_back, "exp", split_axis=0, concat_axis=2, tiled=True)
    combine_map = jnp.where(slot_hot, mixing[:, :, None], 0.0)
    combine_map = jnp.transpose(combine_map, (0, 2, 1)).reshape(tok_here, CAP * expert_count)
    mixture = jnp.dot(
        combine_map,
        returned.reshape(CAP * expert_count, model_width).astype(jnp.float32),
        precision=lax.Precision.HIGHEST,
    )
    return (hidden + mixture).astype(jnp.bfloat16)


def solution(mesh):
    return jax.shard_map(
        body,
        mesh=mesh,
        in_specs=(
            P("ctx", "exp", None),
            P("ctx", "exp"),
            P(None, "ctx"),
            P(None, "ctx"),
            P(),
            P("exp", None, None),
            P("exp", "ctx"),
            P(("ctx", "exp"), None),
            P(),
            P(),
            P(("ctx", "exp"), None),
            P("exp", None, "ctx"),
            P("exp", None, "ctx"),
            P("exp", "ctx", None),
        ),
        out_specs=P(("ctx", "exp"), None),
        check_vma=False,
    )
```

profile of v0, /device:TPU:0, one launch (start us, length us, event | category | flops | bytes accessed | tf_op | source)
XLA Modules:
  0.0 268.8 jit_solution(8497776579315052715)
XLA Ops:
  6.6 0.9 select_reduce_fusion.4
  7.5 0.7 select_reduce_fusion.2
  8.2 1.0 reshape.299
  9.2 1.1 copy.39
  10.3 0.8 pad_maximum_fusion
  11.1 10.3 %all_gather.9 = bf16[576,640]{0,1:T(8,128)(2,1)S(1)} all-gather(bf16[576,160]{0,1:T(8,128)(2,1)S(1)} %pad_maximum_fusion), channel_id=1, replica_groups=mesh['ctx'=4,'exp'=8] {'ctx'}, dimensions={1}, use_global_device_ids=true | all-gather | bytes 921600 | tf_op jit(solution)/shard_map/all_gather | solution.py:90
  21.4 0.1 broadcast_compare_fusion
  21.4 1.6 fusion.16
  23.1 0.1 broadcast_in_dim.113
  23.2 0.5 fusion.39
  23.7 1.1 fusion.8
  24.8 0.1 exp.38
  24.9 0.1 copy.42
  25.0 0.1 reduce_sum.77
  25.1 0.1 mul.121
  25.1 0.1 copy.41
  25.2 0.1 copy.44
  25.3 1.7 fusion.6
  27.0 1.0 fusion.10
  28.1 7.3 %all_gather.10 = bf16[128,2048]{1,0:T(8,128)(2,1)S(1)} all-gather(bf16[32,2048]{1,0:T(8,128)(2,1)S(1)} %bitcast.75), channel_id=1, replica_groups=mesh['ctx'=4,'exp'=8] {'ctx'}, dimensions={0}, use_global_device_ids=true | all-gather | bytes 655360 | tf_op jit(solution)/shard_map/all_gather | solution.py:104
  35.3 4.2 %convolution_convert_fusion.2 = bf16[128,1792]{1,0:T(8,128)(2,1)S(1)} fusion(bf16[128,2048]{1,0:T(8,128)(2,1)S(1)} %all_gather.10, bf16[2048,1792]{1,0:T(8,128)(2,1)} %param.20), kind=kOutput, calls=%fused_computation.5 | convolution fusion | flops 939753472 | bytes 8323072 | tf_op jit(solution)/shard_map/dot_general | solution.py:103
  39.6 0.9 convert_element_type.60
  40.5 0.0 all-reduce.3.cloned.1.call-update
  40.5 0.6 dynamic-slice
  41.1 0.1 convert_reduce_fusion
  41.2 72.6 %all-reduce.3.cloned.1.call-done = bf16[4,8,4,1792]{3,2,1,0:T(4,128)(2,1)} async-done(((bf16[4,8,4,1792]{3,2,1,0:T(4,128)(2,1)}), bf16[4,8,4,1792]{3,2,1,0:T(4,128)(2,1)}) %all-reduce.3.cloned.1.call-update) | async-done | bytes 458768
  113.9 2.1 constant_dynamic-slice_fusion
  115.9 3.3 %all-to-all-start = ((bf16[4,1,4,1792]{3,2,1,0:T(4,128)(2,1)}), bf16[4,1,4,1792]{3,2,1,0:T(4,128)(2,1)S(1)}, u32[]{:S(2)}, u32[]{:S(2)}) async-start(bf16[4,1,4,1792]{3,2,1,0:T(4,128)(2,1)} %constant_dynamic-slice_fusion), calls=%async_computation | async-start | bytes 114688 | tf_op jit(solution)/shard_map/all_to_all | solution.py:112
  119.2 0.0 all-gather.2.cloned.1.call-start
  119.3 0.1 and.112
  119.4 0.1 and.113
  119.5 0.1 eq.95
  119.6 0.1 eq.92
  119.7 0.1 eq.93
  119.8 3.5 %all-to-all-done = bf16[4,1,4,1792]{3,2,1,0:T(4,128)(2,1)S(1)} async-done(((bf16[4,1,4,1792]{3,2,1,0:T(4,128)(2,1)}), bf16[4,1,4,1792]{3,2,1,0:T(4,128)(2,1)S(1)}, u32[]{:S(2)}, u32[]{:S(2)}) %all-to-all-start) | async-done | bytes 57376 | tf_op jit(solution)/shard_map/all_to_all | solution.py:112
  123.3 0.2 multiply_reduce_fusion
  123.5 0.1 multiply_convert_fusion
  123.6 0.3 copy-done.3
  123.9 0.4 convolution_convert_fusion.1
  124.3 0.4 reshape.301
  124.8 26.9 %all_to_all.42 = bf16[16,3,7168]{2,1,0:T(4,128)(2,1)S(1)} all-to-all(bf16[16,3,7168]{2,1,0:T(4,128)(2,1)S(1)} %reshape.301), channel_id=1, replica_groups=mesh['ctx'=4,'exp'=8] {'exp'}, dimensions={0} | all-to-all | bytes 1376256 | tf_op jit(solution)/shard_map/all_to_all | solution.py:137
  151.6 0.6 copy.46
  152.2 1.0 copy.47
  153.2 0.0 all-gather.2.cloned.1.call-update
  153.2 0.2 reduce-scatter.5.cloned.1.call-start
  153.5 23.9 %all-gather.2.cloned.1.call-done = bf16[2,96,7168]{2,1,0:T(8,128)(2,1)} async-done(((bf16[2,24,7168]{2,1,0:T(8,128)(2,1)}), bf16[2,96,7168]{2,1,0:T(8,128)(2,1)}) %all-gather.2.cloned.1.call-update) | async-done | bytes 2752528 | tf_op jit(solution)/shard_map/all_gather | solution.py:145
  177.4 8.6 %fusion.40 = f32[2,96,512]{2,1,0:T(8,128)S(1)} fusion(bf16[2,96,7168]{2,1,0:T(8,128)(2,1)} %all-gather.2.cloned.1.call-done, bf16[2,7168,512]{2,1,0:T(8,128)(2,1)} %param.25), kind=kOutput, calls=%fused_computation.91 | convolution fusion | flops 1409286144 | bytes 17825792 | tf_op jit(solution)/shard_map/end,edf->enf/dot_general | solution.py:146
  186.0 0.0 slice-start.2
  186.0 7.8 %fusion.7 = bf16[2,96,512]{2,1,0:T(8,128)(2,1)S(1)} fusion(bf16[2,96,7168]{2,1,0:T(8,128)(2,1)S(1)} %copy-done.2, bf16[2,7168,512]{2,1,0:T(8,128)(2,1)} %param.26, f32[2,96,512]{2,1,0:T(8,128)S(1)} %fusion.40), kind=kOutput, calls=%fused_computation.15 | convolution fusion | flops 1409875968 | bytes 18022400 | tf_op jit(solution)/shard_map/end,edf->enf/dot_general | solution.py:147
  193.8 2.6 fusion
  196.4 1.8 copy.56
  198.2 0.0 reduce-scatter.5.cloned.1.call-update
  198.2 35.5 %reduce-scatter.5.cloned.1.call-done = bf16[24,14336]{1,0:T(8,128)(2,1)} async-done(((bf16[96,14336]{1,0:T(8,128)(2,1)}), bf16[24,14336]{1,0:T(8,128)(2,1)}) %reduce-scatter.5.cloned.1.call-update) | async-done | bytes 688144
  233.7 2.6 reshape.310
  236.3 5.5 %all-to-all-start.2 = ((bf16[8,3,2,7168]{3,2,1,0:T(2,128)(2,1)}), bf16[8,3,2,7168]{3,2,1,0:T(2,128)(2,1)S(1)}, u32[]{:S(2)}, u32[]{:S(2)}) async-start(bf16[8,3,2,7168]{3,2,1,0:T(2,128)(2,1)} %bitcast.15), calls=%async_computation.2 | async-start | bytes 1376256 | tf_op jit(solution)/shard_map/all_to_all | solution.py:158
  241.8 0.2 fusion.13
  242.0 0.2 select_reduce_fusion
  242.2 0.1 multiply_divide_fusion
  242.3 0.1 select_reduce_fusion.3
  242.4 0.1 select_n.127
  242.5 17.2 %all-to-all-done.2 = bf16[8,3,2,7168]{3,2,1,0:T(2,128)(2,1)S(1)} async-done(((bf16[8,3,2,7168]{3,2,1,0:T(2,128)(2,1)}), bf16[8,3,2,7168]{3,2,1,0:T(2,128)(2,1)S(1)}, u32[]{:S(2)}, u32[]{:S(2)}) %all-to-all-start.2) | async-done | bytes 688160 | tf_op jit(solution)/shard_map/all_to_all | solution.py:158
  259.7 0.5 copy.49
  260.1 0.3 reshape.303
  260.4 1.9 fusion.1
  (41 shorter events, 0.2 us)
Async XLA Ops:
  6.5 20.5 %copy-start = (bf16[16,512,128]{2,1,0:T(8,128)(2,1)S(1)}, bf16[16,512,128]{2,1,0:T(8,128)(2,1)}, u32[]{:S(2)}) copy-start(bf16[16,512,128]{2,1,0:T(8,128)(2,1)} %param.19) | copy-start | bytes 6291460
  6.5 107.3 %all-reduce.3.cloned.1.call-start = ((), (), s32[]{:S(2)}) async-start(), calls=%async_computation.6 | async-start | bytes 917504
  35.3 5.2 %copy-start.8 = (u32[32]{0:T(128)S(1)}, u32[32]{0:T(128)}, u32[]{:S(2)}) copy-start(u32[32]{0:T(128)} %constant.104) | copy-start | bytes 388
  35.3 5.8 %copy-start.6 = (s32[4,8]{1,0:T(4,128)S(1)}, s32[4,8]{1,0:T(4,128)}, u32[]{:S(2)}) copy-start(s32[4,8]{1,0:T(4,128)} %param.24) | copy-start | bytes 388
  35.3 87.9 %copy-start.4 = (bf16[4,7168]{1,0:T(4,128)(2,1)S(1)}, bf16[4,7168]{1,0:T(4,128)(2,1)}, u32[]{:S(2)}) copy-start(bf16[4,7168]{1,0:T(4,128)(2,1)} %param.21) | copy-start | bytes 172036
  35.3 88.1 %copy-start.5 = (f32[7168]{0:T(1024)S(1)}, f32[7168]{0:T(1024)}, u32[]{:S(2)}) copy-start(f32[7168]{0:T(1024)} %param.22) | copy-start | bytes 86020
  115.9 7.3 %all-to-all-start = ((bf16[4,1,4,1792]{3,2,1,0:T(4,128)(2,1)}), bf16[4,1,4,1792]{3,2,1,0:T(4,128)(2,1)S(1)}, u32[]{:S(2)}, u32[]{:S(2)}) async-start(bf16[4,1,4,1792]{3,2,1,0:T(4,128)(2,1)} %constant_dynamic-slice_fusion), calls=%async_computation | async-start | bytes 114688 | tf_op jit(solution)/shard_map/all_to_all | solution.py:112
  119.2 58.2 %all-gather.2.cloned.1.call-start = ((), (), s32[]{:S(2)}) async-start(), calls=%async_computation.4 | async-start | bytes 3440640 | tf_op jit(solution)/shard_map/all_gather | solution.py:145
  123.3 0.7 copy-start.3
  153.2 80.5 %reduce-scatter.5.cloned.1.call-start = ((), (), s32[]{:S(2)}) async-start(), calls=%async_computation.5 | async-start | bytes 3440640
  177.4 8.6 %copy-start.2 = (bf16[2,96,7168]{2,1,0:T(8,128)(2,1)S(1)}, bf16[2,96,7168]{2,1,0:T(8,128)(2,1)}, u32[]{:S(2)}) copy-start(bf16[2,96,7168]{2,1,0:T(8,128)(2,1)} %all-gather.2.cloned.1.call-done) | copy-start | bytes 8257540
  177.4 16.4 %slice-start = ((s8[14680064]{0:T(1024)(128)(4,1)}), s8[4194304]{0:T(1024)(128)(4,1)S(1)}, s32[]{:S(2)}) async-start(s8[14680064]{0:T(1024)(128)(4,1)} %bitcast.63), calls=%async_computation.7 | async-start | bytes 8388608
  177.4 16.4 %slice-start.1 = ((s8[14680064]{0:T(1024)(128)(4,1)}), s8[4194304]{0:T(1024)(128)(4,1)S(1)}, s32[]{:S(2)}) async-start(s8[14680064]{0:T(1024)(128)(4,1)} %bitcast.63), calls=%async_computation.8 | async-start | bytes 8388608
  186.0 7.8 %slice-start.2 = ((s8[14680064]{0:T(1024)(128)(4,1)}), s8[4194304]{0:T(1024)(128)(4,1)S(1)}, s32[]{:S(2)}) async-start(s8[14680064]{0:T(1024)(128)(4,1)} %bitcast.63), calls=%async_computation.9 | async-start | bytes 8388608
  186.0 7.8 %slice-start.3 = ((s8[14680064]{0:T(1024)(128)(4,1)}), s8[2097152]{0:T(1024)(128)(4,1)S(1)}, s32[]{:S(2)}) async-start(s8[14680064]{0:T(1024)(128)(4,1)} %bitcast.63), calls=%async_computation.10 | async-start | bytes 4194304
  198.2 43.6 %copy-start.7 = (bf16[7168,16]{0,1:T(8,128)(2,1)S(1)}, bf16[7168,16]{0,1:T(8,128)(2,1)}, u32[]{:S(2)}) copy-start(bf16[7168,16]{0,1:T(8,128)(2,1)} %param.23) | copy-start | bytes 688132
  233.7 28.6 %copy-start.1 = (bf16[16,512,128]{2,1,0:T(8,128)(2,1)S(1)}, bf16[16,512,128]{2,1,0:T(8,128)(2,1)}, u32[]{:S(2)}) copy-start(bf16[16,512,128]{2,1,0:T(8,128)(2,1)} %param.19) | copy-start | bytes 6291460
  236.3 23.4 %all-to-all-start.2 = ((bf16[8,3,2,7168]{3,2,1,0:T(2,128)(2,1)}), bf16[8,3,2,7168]{3,2,1,0:T(2,128)(2,1)S(1)}, u32[]{:S(2)}, u32[]{:S(2)}) async-start(bf16[8,3,2,7168]{3,2,1,0:T(2,128)(2,1)} %bitcast.15), calls=%async_computation.2 | async-start | bytes 1376256 | tf_op jit(solution)/shard_map/all_to_all | solution.py:158
Sparse Core Ops, SparseCore 0:
  40.6 73.1 all-reduce.2
  153.3 23.9 all-gather.1
  198.3 35.3 reduce-scatter.4
where the time goes:
time: 270 us; the launch traced here: 269 us
  waiting for transfers between devices  153 us (57%)
  blocking collectives  44.4 us (16%)
  matrix products  30.6 us (11%)
  local copies, waits for them, and re-layouts  14.2 us (5%)
  between operations  13.4 us (5%)
  starting transfers between devices  9.06 us (3%)
  other arithmetic  4.49 us (2%)
    unnamed x5, waiting for transfers between devices  108 us
    all_to_all x1, blocking collectives, body(): lax.all_to_all(send_rows.reshape(expert_count, CAP, model_width), 'exp',...  26.9 us
    all_gather x1, waiting for transfers between devices, body(): portion = lax.all_gather(arrived, 'ctx', axis=1, tiled=True)  23.9 us
    all_to_all x1, waiting for transfers between devices, body(): lax.all_to_all(going_back, 'exp', split_axis=0, concat_axis=2, tiled=True)  17.2 us
    all_gather x1, blocking collectives, body(): portion = lax.all_gather(keys_here, 'ctx', axis=1, tiled=True)  10.3 us
    dot_general x1, matrix products, body(): jnp.einsum('end,edf->enf', portion, w_gate, preferred_element_type=jnp.fl...  8.57 us
    dot_general x1, matrix products, body(): jnp.einsum('end,edf->enf', portion, w_up, preferred_element_type=jnp.floa...  7.8 us
    all_gather x1, blocking collectives, body(): lax.all_gather(head_out, 'ctx', axis=0, tiled=True)  7.27 us
  transfers between devices with their start and end apart: 5, of which 5 were waited for; matrix products, arithmetic and copies ran while one was open for 1% of the time, Pallas kernels for 0%

commit v1 on v0

--- a/solution.py
+++ b/solution.py
@@ -134,12 +134,18 @@
     send_rows = jnp.dot(dispatch_map, normed, preferred_element_type=jnp.float32).astype(
         jnp.bfloat16
     )
-    arrived = lax.all_to_all(
-        send_rows.reshape(expert_count, CAP, model_width),
-        "exp",
-        split_axis=0,
-        concat_axis=1,
-        tiled=True,
+    arrived = jnp.concatenate(
+        lax.all_to_all(
+            jnp.stack(
+                jnp.split(
+                    send_rows.reshape(expert_count, CAP, model_width), lax.axis_size("exp"), axis=0
+                )
+            ),
+            "exp",
+            0,
+            0,
+        ),
+        axis=1,
     )
     local_experts = arrived.shape[0]
     portion = lax.all_gather(arrived, "ctx", axis=1, tiled=True)

time: 270 us -> 265 us (0.981)
  blocking collectives: 44.4 us -> 39.3 us
    all_to_all x1, blocking collectives: 26.9 us -> 21.8 us  [body(): lax.all_to_all(jnp.stack(jnp.split(send_rows.reshape(expert_count, CAP, m...]
    unnamed x30 -> x37, local copies, waits for them, and re-layouts: 5.92 us -> 6.41 us
where the time goes in v1:
time: 265 us
  waiting for transfers between devices  153 us (58%)
  blocking collectives  39.3 us (15%)
  matrix products  30.5 us (12%)
  local copies, waits for them, and re-layouts  15.1 us (6%)
  between operations  13.5 us (5%)
  starting transfers between devices  9.06 us (3%)
  other arithmetic  4.49 us (2%)
    unnamed x5, waiting for transfers between devices  108 us
    all_gather x1, waiting for transfers between devices, body(): portion = lax.all_gather(arrived, 'ctx', axis=1, tiled=True)  24 us
    all_to_all x1, blocking collectives, body(): lax.all_to_all(jnp.stack(jnp.split(send_rows.reshape(expert_count, CAP, m...  21.8 us
    all_to_all x1, waiting for transfers between devices, body(): lax.all_to_all(going_back, 'exp', split_axis=0, concat_axis=2, tiled=True)  17.2 us
    all_gather x1, blocking collectives, body(): portion = lax.all_gather(keys_here, 'ctx', axis=1, tiled=True)  10.3 us
    dot_general x1, matrix products, body(): jnp.einsum('end,edf->enf', portion, w_gate, preferred_element_type=jnp.fl...  8.57 us
    dot_general x1, matrix products, body(): jnp.einsum('end,edf->enf', portion, w_up, preferred_element_type=jnp.floa...  7.8 us
    all_gather x1, blocking collectives, body(): lax.all_gather(head_out, 'ctx', axis=0, tiled=True)  7.27 us
  transfers between devices with their start and end apart: 5, of which 5 were waited for; matrix products, arithmetic and copies ran while one was open for 1% of the time, Pallas kernels for 0%

profile of v1, /device:TPU:0, one launch (start us, length us, event | category | flops | bytes accessed | tf_op | source)
XLA Modules:
  0.0 264.8 jit_solution(3717937364256054724)
XLA Ops:
  6.6 0.9 select_reduce_fusion.4
  7.5 0.7 select_reduce_fusion.2
  8.2 1.0 reshape.319
  9.2 1.1 copy.39
  10.3 0.8 pad_maximum_fusion
  11.1 10.3 %all_gather.9 = bf16[576,640]{0,1:T(8,128)(2,1)S(1)} all-gather(bf16[576,160]{0,1:T(8,128)(2,1)S(1)} %pad_maximum_fusion), channel_id=1, replica_groups=mesh['ctx'=4,'exp'=8] {'ctx'}, dimensions={1}, use_global_device_ids=true | all-gather | bytes 921600 | tf_op jit(solution)/shard_map/all_gather | solution.py:90
  21.4 0.1 broadcast_compare_fusion
  21.4 1.6 fusion.16
  23.1 0.1 broadcast_in_dim.113
  23.2 0.5 fusion.40
  23.7 1.1 fusion.8
  24.8 0.1 exp.38
  25.0 0.1 reduce_sum.77
  25.1 0.1 mul.121
  25.2 0.1 copy.44
  25.3 1.7 fusion.6
  27.0 1.0 fusion.10
  28.1 7.3 %all_gather.10 = bf16[128,2048]{1,0:T(8,128)(2,1)S(1)} all-gather(bf16[32,2048]{1,0:T(8,128)(2,1)S(1)} %bitcast.73), channel_id=1, replica_groups=mesh['ctx'=4,'exp'=8] {'ctx'}, dimensions={0}, use_global_device_ids=true | all-gather | bytes 655360 | tf_op jit(solution)/shard_map/all_gather | solution.py:104
  35.3 4.2 %convolution_convert_fusion.2 = bf16[128,1792]{1,0:T(8,128)(2,1)S(1)} fusion(bf16[128,2048]{1,0:T(8,128)(2,1)S(1)} %all_gather.10, bf16[2048,1792]{1,0:T(8,128)(2,1)} %param.20), kind=kOutput, calls=%fused_computation.5 | convolution fusion | flops 939753472 | bytes 8323072 | tf_op jit(solution)/shard_map/dot_general | solution.py:103
  39.6 0.9 convert_element_type.60
  40.5 0.6 dynamic-slice
  41.1 0.1 convert_reduce_fusion
  41.2 72.6 %all-reduce.3.cloned.1.call-done = bf16[4,8,4,1792]{3,2,1,0:T(4,128)(2,1)} async-done(((bf16[4,8,4,1792]{3,2,1,0:T(4,128)(2,1)}), bf16[4,8,4,1792]{3,2,1,0:T(4,128)(2,1)}) %all-reduce.3.cloned.1.call-update) | async-done | bytes 458768
  113.9 2.1 constant_dynamic-slice_fusion
  115.9 3.3 %all-to-all-start = ((bf16[4,1,4,1792]{3,2,1,0:T(4,128)(2,1)}), bf16[4,1,4,1792]{3,2,1,0:T(4,128)(2,1)S(1)}, u32[]{:S(2)}, u32[]{:S(2)}) async-start(bf16[4,1,4,1792]{3,2,1,0:T(4,128)(2,1)} %constant_dynamic-slice_fusion), calls=%async_computation | async-start | bytes 114688 | tf_op jit(solution)/shard_map/all_to_all | solution.py:112
  119.3 0.1 and.112
  119.4 0.1 and.113
  119.5 0.1 eq.95
  119.6 0.1 eq.92
  119.7 0.1 eq.93
  119.8 3.5 %all-to-all-done = bf16[4,1,4,1792]{3,2,1,0:T(4,128)(2,1)S(1)} async-done(((bf16[4,1,4,1792]{3,2,1,0:T(4,128)(2,1)}), bf16[4,1,4,1792]{3,2,1,0:T(4,128)(2,1)S(1)}, u32[]{:S(2)}, u32[]{:S(2)}) %all-to-all-start) | async-done | bytes 57376 | tf_op jit(solution)/shard_map/all_to_all | solution.py:112
  123.3 0.2 multiply_reduce_fusion
  123.5 0.5 copy-done.3
  123.9 0.1 multiply_convert_fusion
  124.0 0.4 convolution_convert_fusion.1
  124.4 0.2 fusion.39
  124.6 0.1 stack.34
  124.7 0.1 stack.33
  124.7 0.1 stack.32
  124.8 0.1 stack.31
  124.9 0.1 stack.30
  125.0 0.1 stack.29
  125.0 0.1 stack.28
  125.6 0.6 copy.46
  126.2 21.8 %all_to_all.29 = bf16[8,2,3,7168]{3,1,2,0:T(2,128)(2,1)S(1)} all-to-all(bf16[8,2,3,7168]{3,1,2,0:T(2,128)(2,1)S(1)} %copy.46), channel_id=1, replica_groups=mesh['ctx'=4,'exp'=8] {'exp'}, dimensions={0} | all-to-all | bytes 1376256 | tf_op jit(solution)/shard_map/all_to_all | solution.py:138
  148.1 1.0 copy.47
  149.1 0.2 reduce-scatter.5.cloned.1.call-start
  149.3 24.0 %all-gather.2.cloned.1.call-done = bf16[2,96,7168]{2,1,0:T(8,128)(2,1)} async-done(((bf16[2,24,7168]{2,1,0:T(8,128)(2,1)}), bf16[2,96,7168]{2,1,0:T(8,128)(2,1)}) %all-gather.2.cloned.1.call-update) | async-done | bytes 2752528 | tf_op jit(solution)/shard_map/all_gather | solution.py:151
  173.3 8.6 %fusion.41 = f32[2,96,512]{2,1,0:T(8,128)S(1)} fusion(bf16[2,96,7168]{2,1,0:T(8,128)(2,1)} %all-gather.2.cloned.1.call-done, bf16[2,7168,512]{2,1,0:T(8,128)(2,1)} %param.25), kind=kOutput, calls=%fused_computation.100 | convolution fusion | flops 1409286144 | bytes 17825792 | tf_op jit(solution)/shard_map/end,edf->enf/dot_general | solution.py:152
  181.9 7.8 %fusion.7 = bf16[2,96,512]{2,1,0:T(8,128)(2,1)S(1)} fusion(bf16[2,96,7168]{2,1,0:T(8,128)(2,1)S(1)} %copy-done.2, bf16[2,7168,512]{2,1,0:T(8,128)(2,1)} %param.26, f32[2,96,512]{2,1,0:T(8,128)S(1)} %fusion.41), kind=kOutput, calls=%fused_computation.15 | convolution fusion | flops 1409875968 | bytes 18022400 | tf_op jit(solution)/shard_map/end,edf->enf/dot_general | solution.py:153
  189.8 2.6 fusion
  192.4 1.8 copy.56
  194.2 35.5 %reduce-scatter.5.cloned.1.call-done = bf16[24,14336]{1,0:T(8,128)(2,1)} async-done(((bf16[96,14336]{1,0:T(8,128)(2,1)}), bf16[24,14336]{1,0:T(8,128)(2,1)}) %reduce-scatter.5.cloned.1.call-update) | async-done | bytes 688144
  229.7 2.6 reshape.331
  232.3 5.5 %all-to-all-start.2 = ((bf16[8,3,2,7168]{3,2,1,0:T(2,128)(2,1)}), bf16[8,3,2,7168]{3,2,1,0:T(2,128)(2,1)S(1)}, u32[]{:S(2)}, u32[]{:S(2)}) async-start(bf16[8,3,2,7168]{3,2,1,0:T(2,128)(2,1)} %bitcast.14), calls=%async_computation.2 | async-start | bytes 1376256 | tf_op jit(solution)/shard_map/all_to_all | solution.py:164
  237.8 0.2 fusion.13
  238.0 0.2 select_reduce_fusion
  238.2 0.1 multiply_divide_fusion
  238.3 0.1 select_reduce_fusion.3
  238.4 0.1 select_n.127
  238.5 17.2 %all-to-all-done.2 = bf16[8,3,2,7168]{3,2,1,0:T(2,128)(2,1)S(1)} async-done(((bf16[8,3,2,7168]{3,2,1,0:T(2,128)(2,1)}), bf16[8,3,2,7168]{3,2,1,0:T(2,128)(2,1)S(1)}, u32[]{:S(2)}, u32[]{:S(2)}) %all-to-all-start.2) | async-done | bytes 688160 | tf_op jit(solution)/shard_map/all_to_all | solution.py:164
  255.6 0.5 copy.49
  256.1 0.3 reshape.324
  256.4 1.9 fusion.1
  (57 shorter events, 1.0 us)
Async XLA Ops:
  6.5 20.5 %copy-start = (bf16[16,512,128]{2,1,0:T(8,128)(2,1)S(1)}, bf16[16,512,128]{2,1,0:T(8,128)(2,1)}, u32[]{:S(2)}) copy-start(bf16[16,512,128]{2,1,0:T(8,128)(2,1)} %param.19) | copy-start | bytes 6291460
  6.5 107.3 %all-reduce.3.cloned.1.call-start = ((), (), s32[]{:S(2)}) async-start(), calls=%async_computation.6 | async-start | bytes 917504
  35.3 5.2 %copy-start.8 = (u32[32]{0:T(128)S(1)}, u32[32]{0:T(128)}, u32[]{:S(2)}) copy-start(u32[32]{0:T(128)} %constant.104) | copy-start | bytes 388
  35.3 5.8 %copy-start.6 = (s32[4,8]{1,0:T(4,128)S(1)}, s32[4,8]{1,0:T(4,128)}, u32[]{:S(2)}) copy-start(s32[4,8]{1,0:T(4,128)} %param.24) | copy-start | bytes 388
  35.3 87.9 %copy-start.4 = (bf16[4,7168]{1,0:T(4,128)(2,1)S(1)}, bf16[4,7168]{1,0:T(4,128)(2,1)}, u32[]{:S(2)}) copy-start(bf16[4,7168]{1,0:T(4,128)(2,1)} %param.21) | copy-start | bytes 172036
  35.3 88.6 %copy-start.5 = (f32[7168]{0:T(1024)S(1)}, f32[7168]{0:T(1024)}, u32[]{:S(2)}) copy-start(f32[7168]{0:T(1024)} %param.22) | copy-start | bytes 86020
  115.9 7.3 %all-to-all-start = ((bf16[4,1,4,1792]{3,2,1,0:T(4,128)(2,1)}), bf16[4,1,4,1792]{3,2,1,0:T(4,128)(2,1)S(1)}, u32[]{:S(2)}, u32[]{:S(2)}) async-start(bf16[4,1,4,1792]{3,2,1,0:T(4,128)(2,1)} %constant_dynamic-slice_fusion), calls=%async_computation | async-start | bytes 114688 | tf_op jit(solution)/shard_map/all_to_all | solution.py:112
  119.2 54.1 %all-gather.2.cloned.1.call-start = ((), (), s32[]{:S(2)}) async-start(), calls=%async_computation.4 | async-start | bytes 3440640 | tf_op jit(solution)/shard_map/all_gather | solution.py:151
  123.3 0.7 copy-start.3
  149.1 80.6 %reduce-scatter.5.cloned.1.call-start = ((), (), s32[]{:S(2)}) async-start(), calls=%async_computation.5 | async-start | bytes 3440640
  173.3 8.6 %copy-start.2 = (bf16[2,96,7168]{2,1,0:T(8,128)(2,1)S(1)}, bf16[2,96,7168]{2,1,0:T(8,128)(2,1)}, u32[]{:S(2)}) copy-start(bf16[2,96,7168]{2,1,0:T(8,128)(2,1)} %all-gather.2.cloned.1.call-done) | copy-start | bytes 8257540
  173.3 16.4 %slice-start = ((s8[14680064]{0:T(1024)(128)(4,1)}), s8[4194304]{0:T(1024)(128)(4,1)S(1)}, s32[]{:S(2)}) async-start(s8[14680064]{0:T(1024)(128)(4,1)} %bitcast.62), calls=%async_computation.7 | async-start | bytes 8388608
  173.3 16.4 %slice-start.1 = ((s8[14680064]{0:T(1024)(128)(4,1)}), s8[4194304]{0:T(1024)(128)(4,1)S(1)}, s32[]{:S(2)}) async-start(s8[14680064]{0:T(1024)(128)(4,1)} %bitcast.62), calls=%async_computation.8 | async-start | bytes 8388608
  181.9 7.8 %slice-start.2 = ((s8[14680064]{0:T(1024)(128)(4,1)}), s8[4194304]{0:T(1024)(128)(4,1)S(1)}, s32[]{:S(2)}) async-start(s8[14680064]{0:T(1024)(128)(4,1)} %bitcast.62), calls=%async_computation.9 | async-start | bytes 8388608
  181.9 7.8 %slice-start.3 = ((s8[14680064]{0:T(1024)(128)(4,1)}), s8[2097152]{0:T(1024)(128)(4,1)S(1)}, s32[]{:S(2)}) async-start(s8[14680064]{0:T(1024)(128)(4,1)} %bitcast.62), calls=%async_computation.10 | async-start | bytes 4194304
  194.1 43.6 %copy-start.7 = (bf16[7168,16]{0,1:T(8,128)(2,1)S(1)}, bf16[7168,16]{0,1:T(8,128)(2,1)}, u32[]{:S(2)}) copy-start(bf16[7168,16]{0,1:T(8,128)(2,1)} %param.23) | copy-start | bytes 688132
  229.7 28.6 %copy-start.1 = (bf16[16,512,128]{2,1,0:T(8,128)(2,1)S(1)}, bf16[16,512,128]{2,1,0:T(8,128)(2,1)}, u32[]{:S(2)}) copy-start(bf16[16,512,128]{2,1,0:T(8,128)(2,1)} %param.19) | copy-start | bytes 6291460
  232.3 23.4 %all-to-all-start.2 = ((bf16[8,3,2,7168]{3,2,1,0:T(2,128)(2,1)}), bf16[8,3,2,7168]{3,2,1,0:T(2,128)(2,1)S(1)}, u32[]{:S(2)}, u32[]{:S(2)}) async-start(bf16[8,3,2,7168]{3,2,1,0:T(2,128)(2,1)} %bitcast.14), calls=%async_computation.2 | async-start | bytes 1376256 | tf_op jit(solution)/shard_map/all_to_all | solution.py:164
Sparse Core Ops, SparseCore 0:
  40.6 73.1 all-reduce.2
  149.2 24.1 all-gather.1
  194.3 35.3 reduce-scatter.4
